TPU v7x, 32 devices: a whole 2x2x4 slice. The times are simulated.
32 devices in a mesh: row: 4 (over y, x), col: 8 (over z, core).
Axes of the slice: x: 2, y: 2, z: 4, core: 2. Of those that a mesh axis runs over, the one named last changes fastest.
Arguments:
- psi: bfloat16 [8192, 8192], P(('row', 'col')), may hold values from -0.125 to 0.125
- hpsi: bfloat16 [8192, 128], P(('row', 'col')), may hold values from -0.796875 to 0.796875
- slab_counts: int32 [32], P(('row', 'col')), may hold values from 1 to 256, 6144 in all
- matrix: float32 [4, 2048, 8, 1024], P('row', None, 'col'), as said below
Outputs:
- reduced: float32 [4, 2048, 8, 1024], P('row', None, 'col')
Inputs may be any that keep to these rules, and one draw needn't show every extreme that they name: Slab k's live plane waves are its first slab_counts[k] slots; the rest are padding; the counts sum to 3 * 256 * 32 // 4. The stored matrix is symmetric.
All inputs are finite; a program needn't handle non-finite values.
Results may differ from a plain program's by a relative error of at most 0.0003.
Values sent between devices are 32-bit elements; how exact they have to be, the bound alone decides.
No kernel may reach another device: no remote copies, remote signals or barrier semaphores. Data moves between devices by JAX's collectives and lax.ppermute only.
A program may use at most 64 MiB of HBM per device.

v0:
```python
import jax
import jax.numpy as jnp
from jax import lax
from jax.sharding import PartitionSpec as P

TILE = 16
HIGH = lax.Precision.HIGHEST


def lower_solve(factor, rhs):
    return lax.linalg.triangular_solve(factor, rhs, left_side=True, lower=True)


def invert_shifted(shifted):
    normal = jnp.dot(shifted.T, shifted, precision=HIGH)
    factor = jnp.linalg.cholesky(normal)
    first = lower_solve(factor, shifted.T)
    return lax.linalg.triangular_solve(factor, first, left_side=True, lower=True, transpose_a=True)


def per_device(psi, hpsi, slab_counts, matrix):
    prow_id = lax.axis_index("row")
    pcol_id = lax.axis_index("col")
    n_row = lax.axis_size("row")
    n_col = lax.axis_size("col")
    slots = psi.shape[0]
    panel = hpsi.shape[1]
    local_rows = matrix.shape[1]
    local_cols = matrix.shape[3]
    tiles_r = local_rows // TILE
    tiles_c = local_cols // TILE
    valid = jnp.arange(slots, dtype=jnp.int32) < slab_counts[0]
    hcols = jnp.where(valid[:, None], hpsi, jnp.zeros_like(hpsi))
    local_r = jnp.arange(local_rows, dtype=jnp.int32)
    local_c = jnp.arange(local_cols, dtype=jnp.int32)
    row_global = (local_r // TILE * n_row + prow_id) * TILE + local_r % TILE
    col_global = (local_c // TILE * n_col + pcol_id) * TILE + local_c % TILE
    partial_value = lax.dot_general(
        psi, hcols, (((0,), (0,)), ((), ())), preferred_element_type=jnp.float32
    )
    whole = lax.psum(partial_value, ("row", "col"))
    prow = lax.dynamic_index_in_dim(
        whole.reshape(tiles_r, n_row, TILE, panel), prow_id, 1, keepdims=False
    ).reshape(local_rows, panel)
    scols = lax.dynamic_index_in_dim(
        whole.reshape(tiles_c, n_col, TILE, panel), pcol_id, 1, keepdims=False
    ).reshape(local_cols, panel)
    span = jnp.arange(panel, dtype=jnp.int32)
    lower_r = jnp.where((row_global >= panel)[:, None], prow, jnp.zeros_like(prow))
    lower_c = jnp.where((col_global >= panel)[:, None], scols, jnp.zeros_like(scols))
    top_select = (row_global[None, :] == panel + span[:, None]).astype(jnp.float32)
    gram_part = jnp.dot(lower_r.T, lower_r, precision=HIGH)
    top_part = jnp.dot(top_select, prow, precision=HIGH)
    gram, top_rows = lax.psum((gram_part, top_part), "row")
    factor = jnp.linalg.cholesky(gram)
    basis_r = lower_solve(factor, lower_r.T).T
    basis_c = lower_solve(factor, lower_c.T).T
    top = lower_solve(factor, top_rows.T).T
    inverse = invert_shifted(jnp.eye(panel, dtype=jnp.float32) - top)
    embed_r = (row_global[:, None] == panel + span[None, :]).astype(jnp.float32)
    embed_c = (col_global[:, None] == panel + span[None, :]).astype(jnp.float32)
    reflect_r = basis_r - embed_r
    reflect_c = basis_c - embed_c
    stored = matrix[0, :, 0, :]
    col_select = (col_global[None, :] == span[:, None]).astype(jnp.float32)
    row_select = (row_global[None, :] == span[:, None]).astype(jnp.float32)
    left = jnp.dot(prow, col_select, precision=HIGH)
    upper = lax.dot_general(row_select, scols, (((0,), (1,)), ((), ())), precision=HIGH)
    inside_r = (row_global < panel)[:, None]
    inside_c = (col_global < panel)[None, :]
    refreshed = jnp.where(
        inside_r & inside_c,
        0.5 * (left + upper),
        jnp.where(inside_c, left, jnp.where(inside_r, upper, stored)),
    )
    zpart = jnp.dot(refreshed, reflect_c, precision=HIGH)
    zrows = lax.psum(zpart, "col")
    upart = lax.dot_general(refreshed, reflect_r, (((0,), (0,)), ((), ())), precision=HIGH)
    ucols = lax.psum(upart, "row")
    wmat = lax.psum(jnp.dot(reflect_r.T, zrows, precision=HIGH), "row")
    core = jnp.dot(jnp.dot(inverse, wmat, precision=HIGH), inverse.T, precision=HIGH)
    first = jnp.dot(reflect_r, jnp.dot(inverse, ucols.T, precision=HIGH), precision=HIGH)
    second = jnp.dot(
        jnp.dot(zrows, inverse.T, precision=HIGH) - jnp.dot(reflect_r, core, precision=HIGH),
        reflect_c.T,
        precision=HIGH,
    )
    return (refreshed - first - second)[None, :, None, :]


def solution(mesh):
    in_specs = (
        P(("row", "col"), None),
        P(("row", "col"), None),
        P(("row", "col")),
        P("row", None, "col", None),
    )
    out_specs = P("row", None, "col", None)
    return jax.shard_map(
        per_device, mesh=mesh, in_specs=in_specs, out_specs=out_specs, check_vma=False
    )
```

profile of v0, /device:TPU:0, one launch (start us, length us, event | category | flops | bytes accessed | tf_op | source)
XLA Modules:
  0.0 421.6 jit_solution(14257435263756658271)
XLA Ops:
  7.2 5.1 %convolution_bitcast_fusion = f32[8192,128]{0,1:T(8,128)} fusion(bf16[256,8192]{1,0:T(8,128)(2,1)} %param.7, bf16[256,128]{1,0:T(8,128)(2,1)} %param.8, pred[256]{0:T(512)(128)(4,1)S(1)} %iota_compare_fusion.9), kind=kOutput, calls=%fused_computation | convolution fusion | flops 536903680 | bytes 8454400 | tf_op jit(solution)/shard_map/dot_general | solution.py:38
  12.6 145.3 %all-reduce.6.cloned.1.call-done = f32[8192,128]{0,1:T(8,128)} async-done(((f32[8192,128]{0,1:T(8,128)}), f32[8192,128]{0,1:T(8,128)}) %all-reduce.6.cloned.1.call-update) | async-done | bytes 4194320 | tf_op jit(solution)/shard_map/psum | solution.py:41
  157.9 5.6 %copy.11 = f32[8192,128]{1,0:T(8,128)} copy(f32[8192,128]{0,1:T(8,128)} %all-reduce.6.cloned.1.call-done) | data formatting | bytes 8388608 | tf_op jit(solution)/shard_map/psum | solution.py:41
  163.4 1.6 broadcast_select_fusion
  165.0 2.4 convolution_bitcast_fusion.1
  167.5 3.6 fusion.10
  171.1 1.3 broadcast_select_fusion.1
  172.4 11.0 %fusion.1 = f32[2048,1024]{1,0:T(8,128)} fusion(f32[2048,1024]{1,0:T(8,128)S(1)} %fusion.10, f32[1,2048,1,1024]{3,2,1,0:T(1,128)} %param.10, pred[1024]{0:T(1024)(128)(4,1)S(1)} %broadcast_compare_fusion.1, pred[2048]{0:T(1024)(128)(4,1)S(1)} %broadcast_compare_fusion, f32[1024,128]{1,0:T(8,128)S(1)} %bitcast.89, s32[2048]{0:T(1024)S(1)} %fusion.60), kind=kOutput, calls=%fused_computation.3 | convolution fusion | flops 3234332672 | bytes 25701376 | tf_op jit(solution)/shard_map/dot_general | solution.py:68
  183.3 1.6 fusion.4
  185.0 23.8 %all-reduce.8.cloned.1.call-done = f32[128,128]{0,1:T(8,128)} async-done(((f32[128,128]{0,1:T(8,128)}), f32[128,128]{0,1:T(8,128)}) %all-reduce.8.cloned.1.call-update) | async-done | bytes 65552 | tf_op jit(solution)/shard_map/psum | solution.py:54
  208.8 0.9 copy.16
  209.7 0.9 fusion.29
  210.5 11.7 %cholesky.44 = f32[128,128]{1,0:T(8,128)S(1)} custom-call(f32[128,128]{1,0:T(8,128)S(1)} %fusion.29), custom_call_target="Cholesky" | custom-call | tf_op jit(solution)/shard_map/jit(cholesky)/cholesky | solution.py:55
  222.3 0.7 compare_reduce_fusion.1
  223.0 0.7 fusion.12
  223.7 9.8 %custom-call.13 = f32[1,128,128]{1,2,0:T(8,128)S(1)} custom-call(f32[1,128,128]{2,1,0:T(8,128)S(1)} %fusion.12), custom_call_target="InvertDiagBlocksLowerTriangular" | custom-call | tf_op jit(solution)/shard_map/triangular_solve | solution.py:11
  234.1 10.1 %fusion.77 = f32[2048,128]{1,0:T(8,128)} fusion(f32[2048,1024]{1,0:T(8,128)} %fusion.1, f32[1024,128]{1,0:T(8,128)S(1)} %convolution_subtract_fusion.2), kind=kOutput, calls=%fused_computation.122 | convolution fusion | flops 3221225472 | bytes 9961472 | tf_op jit(solution)/shard_map/dot_general | solution.py:76
  244.2 1.0 convolution_subtract_fusion.1
  245.2 16.6 %fusion.74 = f32[1024,128]{1,0:T(8,128)} fusion(f32[2048,1024]{1,0:T(8,128)} %fusion.1, f32[2048,128]{1,0:T(8,128)S(1)} %convolution_subtract_fusion.1), kind=kOutput, calls=%fused_computation.119 | convolution fusion | flops 3221225472 | bytes 9961472 | tf_op jit(solution)/shard_map/dot_general | solution.py:78
  261.8 41.8 %all-reduce.10.cloned.1.call-done = f32[2048,128]{1,0:T(8,128)} async-done(((f32[2048,128]{1,0:T(8,128)}), f32[2048,128]{1,0:T(8,128)}) %all-reduce.10.cloned.1.call-update) | async-done | bytes 1048592 | tf_op jit(solution)/shard_map/psum | solution.py:77
  303.7 3.7 fusion.79
  307.3 46.2 %all-reduce.12.cloned.1.call-done = (f32[128,128]{1,0:T(8,128)}, f32[1024,128]{1,0:T(8,128)}, f32[128,128]{1,0:T(8,128)}) async-done(((f32[128,128]{1,0:T(8,128)}, f32[1024,128]{1,0:T(8,128)}, f32[128,128]{1,0:T(8,128)}), (f32[128,128]{1,0:T(8,128)}, f32[1024,128]{1,0:T(8,128)}, f32[128,128]{1,0:T(8,128)})) %all-reduce.12.cloned.1.call-update) | async-done | bytes 655376 | tf_op jit(solution)/shard_map/psum | solution.py:54
  353.6 1.1 fusion.25
  355.1 11.7 %cholesky.55 = f32[128,128]{1,0:T(8,128)S(1)} custom-call(f32[128,128]{1,0:T(8,128)S(1)} %fusion.23), custom_call_target="Cholesky" | custom-call | tf_op jit(solution)/shard_map/jit(cholesky)/cholesky | solution.py:16
  368.0 9.8 %custom-call.14 = f32[1,128,128]{1,2,0:T(8,128)S(1)} custom-call(f32[1,128,128]{2,1,0:T(8,128)S(1)} %fusion.13), custom_call_target="InvertDiagBlocksLowerTriangular" | custom-call | tf_op jit(solution)/shard_map/triangular_solve | solution.py:18
  378.3 1.0 fusion.80
  379.7 1.8 fusion.75
  381.4 7.2 %fusion.76 = f32[2048,1024]{1,0:T(8,128)S(1)} fusion(f32[2048,128]{1,0:T(8,128)S(1)} %convolution_subtract_fusion.1, f32[128,1024]{1,0:T(8,128)S(1)} %fusion.75), kind=kOutput, calls=%fused_computation.121 | convolution fusion | flops 3221225472 | bytes 9961472 | tf_op jit(solution)/shard_map/dot_general | solution.py:82
  388.7 1.0 fusion.78
  389.7 1.0 convolution_subtract_fusion
  390.7 8.0 %subtract_bitcast_fusion = f32[1,2048,1,1024]{3,1,2,0:T(8,128)S(1)} fusion(f32[2048,1024]{1,0:T(8,128)S(1)} %bitcast.83, f32[2048,1024]{1,0:T(8,128)S(1)} %fusion.76, f32[2048,128]{1,0:T(8,128)S(1)} %convolution_subtract_fusion, f32[1024,128]{1,0:T(8,128)S(1)} %convolution_subtract_fusion.2), kind=kOutput, calls=%fused_computation.4 | convolution fusion | flops 3225419776 | bytes 26738688 | tf_op jit(solution)/shard_map/dot_general | solution.py:83
  398.7 16.1 %copy.18 = f32[1,2048,1,1024]{3,2,1,0:T(1,128)} copy(f32[1,2048,1,1024]{3,1,2,0:T(8,128)S(1)} %subtract_bitcast_fusion) | data formatting | bytes 16777216 | tf_op jit(solution)/shard_map/broadcast_in_dim | solution.py:88
  (34 shorter events, 3.3 us)
Async XLA Ops:
  6.5 151.3 %all-reduce.6.cloned.1.call-start = ((), (), s32[]{:S(2)}) async-start(), calls=%async_computation | async-start | bytes 8388608 | tf_op jit(solution)/shard_map/psum | solution.py:41
  12.3 196.4 %all-reduce.8.cloned.1.call-start = ((), (), s32[]{:S(2)}) async-start(), calls=%async_computation.1 | async-start | bytes 131072 | tf_op jit(solution)/shard_map/psum | solution.py:54
  167.5 136.2 %all-reduce.10.cloned.1.call-start = ((), (), s32[]{:S(2)}) async-start(), calls=%async_computation.2 | async-start | bytes 2097152 | tf_op jit(solution)/shard_map/psum | solution.py:77
  244.2 109.4 %all-reduce.12.cloned.1.call-start = ((), (), s32[]{:S(2)}) async-start(), calls=%async_computation.3 | async-start | bytes 1310720 | tf_op jit(solution)/shard_map/psum | solution.py:54
  379.6 9.0 %copy-start = (f32[2048,128]{1,0:T(8,128)S(1)}, f32[2048,128]{1,0:T(8,128)}, u32[]{:S(2)}) copy-start(f32[2048,128]{1,0:T(8,128)} %all-reduce.10.cloned.1.call-done) | copy-start | bytes 3145732
  379.6 11.0 %slice-start = ((s8[8388608]{0:T(1024)(128)(4,1)}), s8[4194304]{0:T(1024)(128)(4,1)S(1)}, s32[]{:S(2)}) async-start(s8[8388608]{0:T(1024)(128)(4,1)} %bitcast.82), calls=%async_computation.4 | async-start | bytes 8388608
  381.4 9.3 %slice-start.1 = ((s8[8388608]{0:T(1024)(128)(4,1)}), s8[4194304]{0:T(1024)(128)(4,1)S(1)}, s32[]{:S(2)}) async-start(s8[8388608]{0:T(1024)(128)(4,1)} %bitcast.82), calls=%async_computation.5 | async-start | bytes 8388608
Sparse Core Ops, SparseCore 0:
  12.9 144.9 all-reduce.5
  167.6 41.1 all-reduce.7
  244.3 59.2 all-reduce.9
  307.5 46.0 all-reduce.11
where the time goes:
time: 428 us; the launch traced here: 422 us
  waiting for transfers between devices  257 us (60%)
  matrix products  77.7 us (18%)
  other arithmetic  49.6 us (12%)
  local copies, waits for them, and re-layouts  22.7 us (5%)
  between operations  14.3 us (3%)
    psum x1, waiting for transfers between devices, per_device(): whole = lax.psum(partial_value, ('row', 'col'))  145 us
    psum x2, waiting for transfers between devices, per_device(): gram, top_rows = lax.psum((gram_part, top_part), 'row')  70 us
    psum x1, waiting for transfers between devices, per_device(): zrows = lax.psum(zpart, 'col')  41.8 us
    dot_general x1, matrix products, per_device(): lax.dot_general(refreshed, reflect_r, (((0,), (0,)), ((), ())), precision...  16.6 us
    broadcast_in_dim x1, local copies, waits for them, and re-layouts, per_device(): return (refreshed - first - second)[None, :, None, :]  16.1 us
    another operation x3, other arithmetic, per_device(): factor = jnp.linalg.cholesky(gram)  12.5 us
    another operation x3, other arithmetic, invert_shifted(): factor = jnp.linalg.cholesky(normal)  12.4 us
    dot_general x1, matrix products, per_device(): lax.dot_general(row_select, scols, (((0,), (1,)), ((), ())), precision=HIGH)  11 us
  transfers between devices with their start and end apart: 4, of which 4 were waited for; matrix products, arithmetic and copies ran while one was open for 8% of the time, Pallas kernels for 0%

commit v1 on v0

--- a/solution.py
+++ b/solution.py
@@ -74,7 +74,7 @@
         jnp.where(inside_c, left, jnp.where(inside_r, upper, stored)),
     )
     zpart = jnp.dot(refreshed, reflect_c, precision=HIGH)
-    zrows = lax.psum(zpart, "col")
+    zrows = jnp.sum(jax.lax.all_gather(zpart, "col"), axis=0)
     upart = lax.dot_general(refreshed, reflect_r, (((0,), (0,)), ((), ())), precision=HIGH)
     ucols = lax.psum(upart, "row")
     wmat = lax.psum(jnp.dot(reflect_r.T, zrows, precision=HIGH), "row")

time: 428 us -> 453 us (1.058)
  waiting for transfers between devices: 257 us -> 279 us
    all_gather x0 -> x1, waiting for transfers between devices: none -> 62.8 us  [per_device(): zrows = jnp.sum(jax.lax.all_gather(zpart, 'col'), axis=0)]
    psum x1 -> x0, waiting for transfers between devices: 41.8 us -> none  [per_device(): zrows = lax.psum(zpart, 'col')]
where the time goes in v1:
time: 453 us; the launch traced here: 446 us
  waiting for transfers between devices  279 us (62%)
  matrix products  76.6 us (17%)
  other arithmetic  53.5 us (12%)
  local copies, waits for them, and re-layouts  22.7 us (5%)
  between operations  14.3 us (3%)
    psum x1, waiting for transfers between devices, per_device(): whole = lax.psum(partial_value, ('row', 'col'))  145 us
    psum x2, waiting for transfers between devices, per_device(): gram, top_rows = lax.psum((gram_part, top_part), 'row')  71.1 us
    all_gather x1, waiting for transfers between devices, per_device(): zrows = jnp.sum(jax.lax.all_gather(zpart, 'col'), axis=0)  62.8 us
    dot_general x1, matrix products, per_device(): lax.dot_general(refreshed, reflect_r, (((0,), (0,)), ((), ())), precision...  16.7 us
    broadcast_in_dim x1, local copies, waits for them, and re-layouts, per_device(): return (refreshed - first - second)[None, :, None, :]  16.1 us
    another operation x3, other arithmetic, per_device(): factor = jnp.linalg.cholesky(gram)  12.5 us
    another operation x3, other arithmetic, invert_shifted(): factor = jnp.linalg.cholesky(normal)  12.4 us
    dot_general x1, matrix products, per_device(): lax.dot_general(row_select, scols, (((0,), (1,)), ((), ())), precision=HIGH)  11 us
  transfers between devices with their start and end apart: 4, of which 4 were waited for; matrix products, arithmetic and copies ran while one was open for 8% of the time, Pallas kernels for 0%

profile of v1, /device:TPU:0, one launch (start us, length us, event | category | flops | bytes accessed | tf_op | source)
XLA Modules:
  0.0 446.5 jit_solution(15138276162760494329)
XLA Ops:
  7.2 5.1 %convolution_bitcast_fusion = f32[8192,128]{0,1:T(8,128)} fusion(bf16[256,8192]{1,0:T(8,128)(2,1)} %param.7, bf16[256,128]{1,0:T(8,128)(2,1)} %param.8, pred[256]{0:T(512)(128)(4,1)S(1)} %iota_compare_fusion.9), kind=kOutput, calls=%fused_computation | convolution fusion | flops 536903680 | bytes 8454400 | tf_op jit(solution)/shard_map/dot_general | solution.py:38
  12.6 145.3 %all-reduce.5.cloned.1.call-done = f32[8192,128]{0,1:T(8,128)} async-done(((f32[8192,128]{0,1:T(8,128)}), f32[8192,128]{0,1:T(8,128)}) %all-reduce.5.cloned.1.call-update) | async-done | bytes 4194320 | tf_op jit(solution)/shard_map/psum | solution.py:41
  157.9 5.6 %copy.11 = f32[8192,128]{1,0:T(8,128)} copy(f32[8192,128]{0,1:T(8,128)} %all-reduce.5.cloned.1.call-done) | data formatting | bytes 8388608 | tf_op jit(solution)/shard_map/psum | solution.py:41
  163.4 1.6 broadcast_select_fusion
  165.0 2.4 convolution_bitcast_fusion.1
  167.5 3.6 fusion.10
  171.1 1.3 broadcast_select_fusion.1
  172.4 11.0 %fusion.1 = f32[2048,1024]{1,0:T(8,128)} fusion(f32[2048,1024]{1,0:T(8,128)S(1)} %fusion.10, f32[1,2048,1,1024]{3,2,1,0:T(1,128)} %param.10, pred[1024]{0:T(1024)(128)(4,1)S(1)} %broadcast_compare_fusion.1, pred[2048]{0:T(1024)(128)(4,1)S(1)} %broadcast_compare_fusion, f32[1024,128]{1,0:T(8,128)S(1)} %bitcast.91, s32[2048]{0:T(1024)S(1)} %fusion.60), kind=kOutput, calls=%fused_computation.3 | convolution fusion | flops 3234332672 | bytes 25701376 | tf_op jit(solution)/shard_map/dot_general | solution.py:68
  183.3 25.4 %all-reduce.7.cloned.1.call-done = f32[128,128]{0,1:T(8,128)} async-done(((f32[128,128]{0,1:T(8,128)}), f32[128,128]{0,1:T(8,128)}) %all-reduce.7.cloned.1.call-update) | async-done | bytes 65552 | tf_op jit(solution)/shard_map/psum | solution.py:54
  208.8 0.9 copy.16
  209.7 0.9 fusion.29
  210.5 11.7 %cholesky.44 = f32[128,128]{1,0:T(8,128)S(1)} custom-call(f32[128,128]{1,0:T(8,128)S(1)} %fusion.29), custom_call_target="Cholesky" | custom-call | tf_op jit(solution)/shard_map/jit(cholesky)/cholesky | solution.py:55
  222.3 0.7 compare_reduce_fusion.1
  223.7 9.8 %custom-call.13 = f32[1,128,128]{1,2,0:T(8,128)S(1)} custom-call(f32[1,128,128]{2,1,0:T(8,128)S(1)} %fusion.12), custom_call_target="InvertDiagBlocksLowerTriangular" | custom-call | tf_op jit(solution)/shard_map/triangular_solve | solution.py:11
  234.1 10.1 %fusion.77 = f32[2048,128]{1,0:T(8,128)} fusion(f32[2048,1024]{1,0:T(8,128)} %fusion.1, f32[1024,128]{1,0:T(8,128)S(1)} %convolution_subtract_fusion.2), kind=kOutput, calls=%fused_computation.122 | convolution fusion | flops 3221225472 | bytes 9961472 | tf_op jit(solution)/shard_map/dot_general | solution.py:76
  244.3 1.7 fusion.4
  246.0 1.0 convolution_subtract_fusion.1
  246.9 16.7 %fusion.74 = f32[1024,128]{1,0:T(8,128)} fusion(f32[2048,1024]{1,0:T(8,128)} %fusion.1, f32[2048,128]{1,0:T(8,128)S(1)} %convolution_subtract_fusion.1), kind=kOutput, calls=%fused_computation.119 | convolution fusion | flops 3221225472 | bytes 9961472 | tf_op jit(solution)/shard_map/dot_general | solution.py:78
  263.6 62.8 %all-gather.3.cloned.1.call-done = f32[16384,128]{1,0:T(8,128)} async-done(((f32[2048,128]{1,0:T(8,128)}), f32[16384,128]{1,0:T(8,128)}) %all-gather.3.cloned.1.call-update) | async-done | bytes 8388624 | tf_op jit(solution)/shard_map/all_gather | solution.py:77
  326.4 3.9 reduce_sum.9
  330.3 2.4 fusion.79
  332.8 45.6 %all-reduce.9.cloned.1.call-done = (f32[128,128]{1,0:T(8,128)}, f32[1024,128]{1,0:T(8,128)}, f32[128,128]{1,0:T(8,128)}) async-done(((f32[128,128]{1,0:T(8,128)}, f32[1024,128]{1,0:T(8,128)}, f32[128,128]{1,0:T(8,128)}), (f32[128,128]{1,0:T(8,128)}, f32[1024,128]{1,0:T(8,128)}, f32[128,128]{1,0:T(8,128)})) %all-reduce.9.cloned.1.call-update) | async-done | bytes 655376 | tf_op jit(solution)/shard_map/psum | solution.py:54
  378.5 1.1 fusion.25
  380.0 11.7 %cholesky.55 = f32[128,128]{1,0:T(8,128)S(1)} custom-call(f32[128,128]{1,0:T(8,128)S(1)} %fusion.23), custom_call_target="Cholesky" | custom-call | tf_op jit(solution)/shard_map/jit(cholesky)/cholesky | solution.py:16
  392.9 9.8 %custom-call.14 = f32[1,128,128]{1,2,0:T(8,128)S(1)} custom-call(f32[1,128,128]{2,1,0:T(8,128)S(1)} %fusion.13), custom_call_target="InvertDiagBlocksLowerTriangular" | custom-call | tf_op jit(solution)/shard_map/triangular_solve | solution.py:18
  403.2 1.0 fusion.78
  404.3 1.0 fusion.80
  405.6 1.8 fusion.75
  407.4 7.2 %fusion.76 = f32[2048,1024]{1,0:T(8,128)S(1)} fusion(f32[2048,128]{1,0:T(8,128)S(1)} %convolution_subtract_fusion.1, f32[128,1024]{1,0:T(8,128)S(1)} %fusion.75), kind=kOutput, calls=%fused_computation.121 | convolution fusion | flops 3221225472 | bytes 9961472 | tf_op jit(solution)/shard_map/dot_general | solution.py:82
  414.6 1.0 convolution_subtract_fusion
  415.6 8.0 %subtract_bitcast_fusion = f32[1,2048,1,1024]{3,1,2,0:T(8,128)S(1)} fusion(f32[2048,1024]{1,0:T(8,128)S(1)} %bitcast.84, f32[2048,1024]{1,0:T(8,128)S(1)} %fusion.76, f32[2048,128]{1,0:T(8,128)S(1)} %convolution_subtract_fusion, f32[1024,128]{1,0:T(8,128)S(1)} %convolution_subtract_fusion.2), kind=kOutput, calls=%fused_computation.4 | convolution fusion | flops 3225419776 | bytes 26738688 | tf_op jit(solution)/shard_map/dot_general | solution.py:83
  423.6 16.1 %copy.18 = f32[1,2048,1,1024]{3,2,1,0:T(1,128)} copy(f32[1,2048,1,1024]{3,1,2,0:T(8,128)S(1)} %subtract_bitcast_fusion) | data formatting | bytes 16777216 | tf_op jit(solution)/shard_map/broadcast_in_dim | solution.py:88
  (33 shorter events, 4.0 us)
Async XLA Ops:
  6.5 151.3 %all-reduce.5.cloned.1.call-start = ((), (), s32[]{:S(2)}) async-start(), calls=%async_computation | async-start | bytes 8388608 | tf_op jit(solution)/shard_map/psum | solution.py:41
  12.3 196.4 %all-reduce.7.cloned.1.call-start = ((), (), s32[]{:S(2)}) async-start(), calls=%async_computation.1 | async-start | bytes 131072 | tf_op jit(solution)/shard_map/psum | solution.py:54
  167.5 159.0 %all-gather.3.cloned.1.call-start = ((), (), s32[]{:S(2)}) async-start(), calls=%async_computation.2 | async-start | bytes 9437184 | tf_op jit(solution)/shard_map/all_gather | solution.py:77
  244.3 134.2 %all-reduce.9.cloned.1.call-start = ((), (), s32[]{:S(2)}) async-start(), calls=%async_computation.3 | async-start | bytes 1310720 | tf_op jit(solution)/shard_map/psum | solution.py:54
  405.6 10.0 %slice-start = ((s8[8388608]{0:T(1024)(128)(4,1)}), s8[4194304]{0:T(1024)(128)(4,1)S(1)}, s32[]{:S(2)}) async-start(s8[8388608]{0:T(1024)(128)(4,1)} %bitcast.83), calls=%async_computation.4 | async-start | bytes 8388608
  407.4 8.2 %slice-start.1 = ((s8[8388608]{0:T(1024)(128)(4,1)}), s8[4194304]{0:T(1024)(128)(4,1)S(1)}, s32[]{:S(2)}) async-start(s8[8388608]{0:T(1024)(128)(4,1)} %bitcast.83), calls=%async_computation.5 | async-start | bytes 8388608
Sparse Core Ops, SparseCore 0:
  12.9 144.9 all-reduce.4
  167.6 41.1 all-reduce.6
  244.4 82.0 all-gather.2
  332.9 45.4 all-reduce.8
